TPU v7x, 32 devices: a whole 2x2x4 slice. The times are simulated.
32 devices in a mesh: pool: 16 (over z, y, x), con: 2 (over core).
Axes of the slice: x: 2, y: 2, z: 4, core: 2. Of those that a mesh axis runs over, the one named last changes fastest.
Arguments:
- pool_feat: bfloat16 [8192, 64], P('pool'), may hold values from -5 to 5
- contract_feat: bfloat16 [8192, 64], P('con'), may hold values from -5 to 5
- supply: float32 [8192], P('pool'), may hold values from 0.3 to 4
- caps: int32 [8192], P('con'), may hold values from 1 to 16
- eligible: int32 [64, 64], P('pool', 'con'), may hold values from 0 to 1, as said below
- grad_log_pool: float32 [8192], P('pool'), may hold values from -48 to 48
- grad_log_contract: float32 [8192], P('con'), may hold values from -48 to 48
Outputs:
- pool_grad: float32 [8192, 64], P('pool')
- contract_grad: float32 [8192, 64], P('con')
Inputs may be any that keep to these rules, and one draw needn't show every extreme that they name: `eligible`: values are 0 or 1; every row of tiles and every column of tiles holds at least one 1.
All inputs are finite; a program needn't handle non-finite values.
Results may differ from a plain program's by a relative error of at most 0.0026.
Values sent between devices are 32-bit elements; how exact they have to be, the bound alone decides.
A program may use at most 64 MiB of HBM per device.

v0:
```python
import jax
import jax.numpy as jnp
from jax import lax
from jax.sharding import PartitionSpec as P

ITERS = 2


HIGHEST_PRECISION = lax.Precision.HIGHEST


def kernel_tile(pool_feat, feat_block, mask_block, tile_side):
    scores = jnp.dot(pool_feat, feat_block.T, preferred_element_type=jnp.float32) * 0.125
    values = jnp.exp(scores)
    row_count, col_count = values.shape
    shaped = (
        values.reshape(row_count // tile_side, tile_side, col_count // tile_side, tile_side)
        * mask_block.astype(jnp.float32)[:, None, :, None]
    )
    return shaped.reshape(row_count, col_count)


def forward_scale(summed, demand):
    return demand / summed


def last_adjoint(summed, gradient, contract_scale, demand):
    return -(gradient / contract_scale + summed) * contract_scale * contract_scale / demand


def inner_adjoint(summed, contract_scale, demand):
    return -summed * contract_scale * contract_scale / demand


def column_step(partial_sum, update, others):
    summed = lax.psum(partial_sum, "pool")
    return update(summed, *others)


def row_step(partial_sum):
    return lax.psum(partial_sum, "con")


def shards(pool_feat, contract_feat, supply, caps, eligible, grad_log_pool, grad_log_contract):
    row_count = pool_feat.shape[0]
    col_count = contract_feat.shape[0]
    width_feat = contract_feat.shape[1]
    tile_side = row_count // eligible.shape[0]
    block_width = min(1024, col_count)
    blocks = col_count // block_width
    feat_blocks = contract_feat.reshape(blocks, block_width, width_feat)
    mask_blocks = eligible.reshape(eligible.shape[0], blocks, block_width // tile_side).transpose(
        1, 0, 2
    )
    demand = caps.astype(jnp.float32)

    def column_sums(weights):

        def column_per_block(entries):
            kernel = kernel_tile(pool_feat, entries[0], entries[1], tile_side)
            return jnp.dot(weights, kernel, precision=HIGHEST_PRECISION)

        return lax.map(column_per_block, (feat_blocks, mask_blocks)).reshape(col_count)

    def row_sums(weights):
        weight_blocks = weights.reshape(blocks, block_width)

        def row_per_block(summed, entries):
            kernel = kernel_tile(pool_feat, entries[0], entries[1], tile_side)
            return (summed + jnp.dot(kernel, entries[2], precision=HIGHEST_PRECISION), None)

        summed, _ = lax.scan(
            row_per_block,
            jnp.zeros((row_count,), jnp.float32),
            (feat_blocks, mask_blocks, weight_blocks),
        )
        return summed

    pool_scale = jnp.ones((row_count,), jnp.float32)
    earlier = []
    contract_scales = []
    row_results = []
    for iteration in range(ITERS):
        earlier.append(pool_scale)
        contract_scale = column_step(column_sums(pool_scale), forward_scale, (demand,))
        row_total = row_step(row_sums(contract_scale))
        pool_scale = supply / row_total
        contract_scales.append(contract_scale)
        row_results.append(row_total)
    row_adj = -grad_log_pool / row_results[-1]
    left_parts = []
    right_parts = []
    for iteration in reversed(range(ITERS)):
        contract_scale = contract_scales[iteration]
        if iteration == ITERS - 1:
            col_adj = column_step(
                column_sums(row_adj), last_adjoint, (grad_log_contract, contract_scale, demand)
            )
        else:
            col_adj = column_step(column_sums(row_adj), inner_adjoint, (contract_scale, demand))
        left_parts += [row_adj, earlier[iteration]]
        right_parts += [contract_scale, col_adj]
        if iteration > 0:
            pool_adj = row_step(row_sums(col_adj))
            row_adj = -pool_adj * earlier[iteration] / row_results[iteration - 1]
    left_mat = jnp.stack(left_parts, axis=1)
    right_blocks = jnp.stack(right_parts, axis=1).reshape(blocks, block_width, 2 * ITERS)

    def final_block(carried, entries):
        kernel = kernel_tile(pool_feat, entries[0], entries[1], tile_side)
        weights = jnp.dot(left_mat, entries[2].T, precision=HIGHEST_PRECISION)
        product = (kernel * weights).astype(jnp.bfloat16)
        carried = carried + jnp.dot(product, entries[0], preferred_element_type=jnp.float32) * 0.125
        column_part = (
            lax.dot_general(
                product, pool_feat, (((0,), (0,)), ((), ())), preferred_element_type=jnp.float32
            )
            * 0.125
        )
        return (carried, column_part)

    pool_part, column_blocks = lax.scan(
        final_block,
        jnp.zeros((row_count, width_feat), jnp.float32),
        (feat_blocks, mask_blocks, right_blocks),
    )
    contract_part = column_blocks.reshape(col_count, width_feat)
    pool_grad = lax.psum(pool_part, "con")
    shared = lax.psum_scatter(contract_part, "pool", scatter_dimension=0, tiled=True)
    contract_grad = lax.all_gather(shared, "pool", axis=0, tiled=True)
    return (pool_grad, contract_grad)


def solution(mesh):
    placed = (
        P("pool", None),
        P("con", None),
        P("pool"),
        P("con"),
        P("pool", "con"),
        P("pool"),
        P("con"),
    )
    return jax.shard_map(
        shards,
        mesh=mesh,
        in_specs=placed,
        out_specs=(P("pool", None), P("con", None)),
        check_vma=False,
    )
```

profile of v0, /device:TPU:0, one launch (start us, length us, event | category | flops | bytes accessed | tf_op | source)
XLA Modules:
  0.0 604.7 jit_solution(16692623797993612276)
XLA Ops:
  8.1 2.4 copy.17
  11.2 15.3 %while.86 = (s32[]{:T(128)}, f32[4,1024]{1,0:T(4,128)S(1)}, bf16[4,1024,64]{2,1,0:T(8,128)(2,1)}, bf16[512,64]{0,1:T(8,128)(2,1)}, s32[4,4,8]{2,1,0:T(4,128)S(1)}, /*index=5*/s32[]{:T(128)}, s32[]{:T(128)}) while((s32[]{:T(128)}, f32[4,1024]{1,0:T(4,128)S(1)}, bf16[4,1024,64]{2,1,0:T(8,128)(2,1)}, bf16[512,64]{0,1:T(8,128)(2,1)}, ...), condition=%wide.region_1.2_spmd, body=%wide.region_0.1_spmd.sunk | while | flops 74448928 | bytes 8729813 | solution.py:63
  11.3 1.4 fusion.169
  13.1 1.9 fusion.170
  16.9 1.9 fusion.170
  18.9 1.4 fusion.169
  20.7 1.9 fusion.170
  24.5 1.9 fusion.170
  26.6 78.6 %psum.56 = f32[4096]{0:T(1024)S(1)} all-reduce(f32[4096]{0:T(1024)S(1)} %bitcast.374), channel_id=1, replica_groups=mesh['pool'=16,'con'=2] {'pool'}, use_global_device_ids=true, to_apply=%region_2.3 | all-reduce | flops 4096 | bytes 32768 | tf_op jit(solution)/shard_map/psum | solution.py:36
  105.2 13.1 %while.90 = (s32[]{:T(128)}, f32[512]{0:T(512)S(1)}, bf16[4,1024,64]{2,1,0:T(8,128)(2,1)}, bf16[512,64]{0,1:T(8,128)(2,1)}, s32[4,4,8]{2,1,0:T(4,128)S(1)}, /*index=5*/f32[4,1024]{1,0:T(4,128)S(1)}, s32[]{:T(128)}, s32[]{:T(128)}) while((s32[]{:T(128)}, f32[512]{0:T(512)S(1)}, bf16[4,1024,64]{2,1,0:T(8,128)(2,1)}, ...), condition=%wide.region_4.5_spmd.clone, body=%wide.region_3.4_spmd.clone.sunk | while | flops 74449952 | bytes 8729831 | solution.py:72
  105.2 1.4 fusion.189
  107.0 1.4 fusion.190
  110.3 1.4 fusion.190
  113.6 1.4 fusion.190
  116.9 1.4 fusion.190
  118.3 2.5 psum.57
  120.8 16.1 %while.87 = (s32[]{:T(128)}, f32[4,1024]{1,0:T(4,128)S(1)}, bf16[4,1024,64]{2,1,0:T(8,128)(2,1)}, bf16[512,64]{0,1:T(8,128)(2,1)}, s32[4,4,8]{2,1,0:T(4,128)S(1)}, /*index=5*/f32[512]{0:T(512)S(1)}, s32[]{:T(128)}, s32[]{:T(128)}) while((s32[]{:T(128)}, f32[4,1024]{1,0:T(4,128)S(1)}, bf16[4,1024,64]{2,1,0:T(8,128)(2,1)}, ...), condition=%wide.region_7.8_spmd, body=%wide.region_6.7_spmd.sunk | while | flops 74448928 | bytes 8731869 | solution.py:63
  122.6 2.1 fusion.175
  126.7 2.1 fusion.175
  130.7 2.1 fusion.175
  134.7 2.1 fusion.175
  136.9 71.7 %psum.58 = f32[4096]{0:T(1024)S(1)} all-reduce(f32[4096]{0:T(1024)S(1)} %bitcast.375), channel_id=1, replica_groups=mesh['pool'=16,'con'=2] {'pool'}, use_global_device_ids=true, to_apply=%region_8.9 | all-reduce | flops 4096 | bytes 32768 | tf_op jit(solution)/shard_map/psum | solution.py:36
  208.7 13.2 %while.91 = (s32[]{:T(128)}, f32[512]{0:T(512)S(1)}, bf16[4,1024,64]{2,1,0:T(8,128)(2,1)}, bf16[512,64]{0,1:T(8,128)(2,1)}, s32[4,4,8]{2,1,0:T(4,128)S(1)}, /*index=5*/f32[4,1024]{1,0:T(4,128)S(1)}, s32[]{:T(128)}, s32[]{:T(128)}) while((s32[]{:T(128)}, f32[512]{0:T(512)S(1)}, bf16[4,1024,64]{2,1,0:T(8,128)(2,1)}, ...), condition=%wide.region_10.11_spmd.clone, body=%wide.region_9.10_spmd.clone.sunk | while | flops 74449952 | bytes 8729831 | solution.py:72
  208.7 1.4 fusion.194
  210.5 1.4 fusion.195
  213.8 1.4 fusion.195
  215.3 1.4 fusion.194
  217.1 1.4 fusion.195
  220.4 1.4 fusion.195
  221.8 2.5 psum.59
  224.3 16.1 %while.88 = (s32[]{:T(128)}, f32[4,1024]{1,0:T(4,128)S(1)}, bf16[4,1024,64]{2,1,0:T(8,128)(2,1)}, bf16[512,64]{0,1:T(8,128)(2,1)}, s32[4,4,8]{2,1,0:T(4,128)S(1)}, /*index=5*/f32[512]{0:T(512)S(1)}, s32[]{:T(128)}, s32[]{:T(128)}) while((s32[]{:T(128)}, f32[4,1024]{1,0:T(4,128)S(1)}, bf16[4,1024,64]{2,1,0:T(8,128)(2,1)}, ...), condition=%wide.region_13.14_spmd, body=%wide.region_12.13_spmd.sunk | while | flops 74448928 | bytes 8731869 | solution.py:63
  224.4 1.4 fusion.179
  226.2 2.1 fusion.180
  230.2 2.1 fusion.180
  234.2 2.1 fusion.180
  238.2 2.1 fusion.180
  240.4 71.9 %psum.60 = f32[4096]{0:T(1024)S(1)} all-reduce(f32[4096]{0:T(1024)S(1)} %bitcast.376), channel_id=1, replica_groups=mesh['pool'=16,'con'=2] {'pool'}, use_global_device_ids=true, to_apply=%region_14.15 | all-reduce | flops 4096 | bytes 32768 | tf_op jit(solution)/shard_map/psum | solution.py:36
  312.4 13.2 %while.92 = (s32[]{:T(128)}, f32[512]{0:T(512)S(1)}, bf16[4,1024,64]{2,1,0:T(8,128)(2,1)}, bf16[512,64]{0,1:T(8,128)(2,1)}, s32[4,4,8]{2,1,0:T(4,128)S(1)}, /*index=5*/f32[4,1024]{1,0:T(4,128)S(1)}, s32[]{:T(128)}, s32[]{:T(128)}) while((s32[]{:T(128)}, f32[512]{0:T(512)S(1)}, bf16[4,1024,64]{2,1,0:T(8,128)(2,1)}, ...), condition=%wide.region_16.17_spmd.clone, body=%wide.region_15.16_spmd.clone.sunk | while | flops 74449952 | bytes 8729831 | solution.py:72
  314.2 1.4 fusion.200
  315.7 1.4 fusion.199
  317.5 1.4 fusion.200
  320.8 1.4 fusion.200
  324.1 1.4 fusion.200
  325.5 2.5 psum.61
  328.0 16.0 %while.89 = (s32[]{:T(128)}, f32[4,1024]{1,0:T(4,128)S(1)}, bf16[4,1024,64]{2,1,0:T(8,128)(2,1)}, bf16[512,64]{0,1:T(8,128)(2,1)}, s32[4,4,8]{2,1,0:T(4,128)S(1)}, /*index=5*/f32[512]{0:T(512)S(1)}, s32[]{:T(128)}, s32[]{:T(128)}) while((s32[]{:T(128)}, f32[4,1024]{1,0:T(4,128)S(1)}, bf16[4,1024,64]{2,1,0:T(8,128)(2,1)}, ...), condition=%wide.region_19.20_spmd, body=%wide.region_18.19_spmd.sunk | while | flops 74448928 | bytes 8731869 | solution.py:63
  329.8 2.1 fusion.185
  333.8 2.1 fusion.185
  337.9 2.1 fusion.185
  341.9 2.1 fusion.185
  344.1 71.7 %psum.62 = f32[4096]{0:T(1024)S(1)} all-reduce(f32[4096]{0:T(1024)S(1)} %bitcast.377), channel_id=1, replica_groups=mesh['pool'=16,'con'=2] {'pool'}, use_global_device_ids=true, to_apply=%region_20.21 | all-reduce | flops 4096 | bytes 32768 | tf_op jit(solution)/shard_map/psum | solution.py:36
  416.1 47.5 %while.93 = (s32[]{:T(128)}, f32[512,64]{0,1:T(8,128)S(1)}, f32[4,1024,64]{1,0,2:T(4,128)}, bf16[4,1024,64]{2,1,0:T(8,128)(2,1)}, bf16[512,64]{0,1:T(8,128)(2,1)...) while((s32[]{:T(128)}, f32[512,64]{0,1:T(8,128)S(1)}, ...), condition=%wide.region_22.23_spmd.clone, body=%wide.region_21.22_spmd.clone.sunk | while | flops 228753440 | bytes 14051095 | solution.py:122
  417.9 2.1 fusion.210
  420.7 5.9 dynamic_update_slice.27
  429.8 2.1 fusion.210
  432.6 5.9 dynamic_update_slice.27
  441.6 2.1 fusion.210
  444.5 5.9 dynamic_update_slice.27
  453.5 2.1 fusion.210
  456.4 5.9 dynamic_update_slice.27
  463.6 2.9 copy.41
  466.5 74.6 %reduce-scatter.2.cloned.1.call-done = f32[256,64]{0,1:T(8,128)} async-done(((f32[4096,64]{0,1:T(8,128)}), f32[256,64]{0,1:T(8,128)}) %reduce-scatter.2.cloned.1.call-update) | async-done | bytes 65552 | tf_op jit(solution)/shard_map/reduce_scatter | solution.py:129
  541.7 51.8 %all-gather.2.cloned.1.call-done = f32[4096,64]{0,1:T(8,128)} async-done(((f32[256,64]{0,1:T(8,128)}), f32[4096,64]{0,1:T(8,128)}) %all-gather.2.cloned.1.call-update) | async-done | bytes 1048592 | tf_op jit(solution)/shard_map/all_gather | solution.py:130
  593.5 1.6 copy.171
  595.0 2.3 copy.172
  (214 shorter events, 58.9 us)
Async XLA Ops:
  8.0 533.1 %reduce-scatter.2.cloned.1.call-start = ((), (), s32[]{:S(2)}) async-start(), calls=%async_computation.2 | async-start | bytes 1114112 | tf_op jit(solution)/shard_map/reduce_scatter | solution.py:129
  11.2 93.9 %copy-start.2 = (s32[4096]{0:T(1024)S(1)}, s32[4096]{0:T(1024)}, u32[]{:S(2)}) copy-start(s32[4096]{0:T(1024)} %param.26) | copy-start | bytes 49156
  105.2 15.6 %copy-start.4 = (f32[512]{0:T(512)S(1)}, f32[512]{0:T(512)}, u32[]{:S(2)}) copy-start(f32[512]{0:T(512)} %param.25) | copy-start | bytes 6148
  208.7 15.7 %copy-start.5 = (f32[512]{0:T(512)S(1)}, f32[512]{0:T(512)}, u32[]{:S(2)}) copy-start(f32[512]{0:T(512)} %param.28) | copy-start | bytes 6148
  224.3 88.0 %copy-start.3 = (f32[4096]{0:T(1024)S(1)}, f32[4096]{0:T(1024)}, u32[]{:S(2)}) copy-start(f32[4096]{0:T(1024)} %param.29) | copy-start | bytes 49156
  417.9 2.2 copy-start
  429.7 2.2 copy-start
  441.6 2.2 copy-start
  453.5 2.2 copy-start
  463.6 77.6 %copy-start.1 = (f32[512,64]{0,1:T(8,128)}, f32[512,64]{0,1:T(8,128)S(1)}, u32[]{:S(2)}) copy-start(f32[512,64]{0,1:T(8,128)S(1)} %get-tuple-element.271) | copy-start | bytes 393220
  466.5 127.0 %all-gather.2.cloned.1.call-start = ((), (), s32[]{:S(2)}) async-start(), calls=%async_computation.3 | async-start | bytes 1114112 | tf_op jit(solution)/shard_map/all_gather | solution.py:130
  541.1 52.4 %all-reduce.2.cloned.1.call-start = ((), (), s32[]{:S(2)}) async-start(), calls=%async_computation.1 | async-start | bytes 262144 | tf_op jit(solution)/shard_map/psum | solution.py:128
Sparse Core Ops, SparseCore 0:
  466.6 74.4 reduce-scatter.1
  543.8 49.6 all-gather.1
Sparse Core Ops, SparseCore 1:
  544.5 14.0 all-reduce.1
where the time goes:
time: 606 us; the launch traced here: 605 us
  blocking collectives  301 us (50%)
  waiting for transfers between devices  127 us (21%)
  matrix products  109 us (18%)
  local copies, waits for them, and re-layouts  49 us (8%)
  between operations  15.7 us (3%)
    psum x4, blocking collectives, column_step(): summed = lax.psum(partial_sum, 'pool')  294 us
    reduce_scatter x1, waiting for transfers between devices, shards(): lax.psum_scatter(contract_part, 'pool', scatter_dimension=0, tiled=True)  74.6 us
    all_gather x1, waiting for transfers between devices, shards(): contract_grad = lax.all_gather(shared, 'pool', axis=0, tiled=True)  51.8 us
    dot_general x32, matrix products, kernel_tile(): jnp.dot(pool_feat, feat_block.T, preferred_element_type=jnp.float32) * 0.125  43.5 us
    dot_general x16, matrix products, column_per_block(): return jnp.dot(weights, kernel, precision=HIGHEST_PRECISION)  33.1 us
    dynamic_update_slice x8, local copies, waits for them, and re-layouts, shards(): lax.scan(final_block, jnp.zeros((row_count, width_feat), jnp.float32), (f...  24.5 us
    dot_general x12, matrix products, row_per_block(): jnp.dot(kernel, entries[2], precision=HIGHEST_PRECISION)  17.4 us
  transfers between devices with their start and end apart: 3, of which 2 were waited for; matrix products, arithmetic and copies ran while one was open for 0% of the time, Pallas kernels for 0%

commit v1 on v0

v1 whole, which is shorter than its diff:
```python
import functools
import math

import jax
import jax.numpy as jnp
from jax import lax
from jax.experimental import pallas as pl
from jax.experimental.pallas import tpu as pltpu
from jax.sharding import PartitionSpec as P

MESH = pl.DeviceIdType.MESH
F32 = jnp.float32
BF16 = jnp.bfloat16
INNER = 4
SCALE = 0.125
NN = (((1,), (0,)), ((), ()))
NT = (((1,), (1,)), ((), ()))
TN = (((0,), (0,)), ((), ()))


def dot(a, b, dims):
    return lax.dot_general(a, b, dims, preferred_element_type=F32)


def parts(x):
    high = x.astype(BF16).astype(F32)
    return high, x - high


def split_rows(x):
    high, low = parts(x)
    row = lax.broadcasted_iota(jnp.int32, (8, x.shape[1]), 0)
    return jnp.where(row == 0, high, jnp.where(row == 1, low, 0.0)).astype(BF16)


def fill_rows(ref, rows):
    for at, row in enumerate(rows):
        ref[at : at + 1, :] = row
    ref[len(rows) :, :] = jnp.zeros((ref.shape[0] - len(rows), ref.shape[1]), F32)


def left_rows(vectors):
    rows = []
    for x in vectors:
        high, low = parts(x)
        rows += [high, high, low]
    return rows


def right_rows(vectors):
    rows = []
    for x in vectors:
        high, low = parts(x)
        rows += [high, low, high]
    return rows


def kernel(
    pools, cons,
    pf_ref, cf_ref, supply_ref, caps_ref, mask_ref, glp_ref, glc_ref,
    pool_out, contract_out,
    kmat, kpeer, pft, pft_in, mask_in, col_part, col_in, mid_part, mid_in,
    row_part, row_in, row_vec, row_vec_in, vee, cbar, left, right,
    pg_part, pg_in, rs_part, rs_in, gathered,
    col_sem, mid_sem, row_sem, vec_sem, feat_sem, mask_sem, pg_sem, rs_sem, agz_sem, agp_sem,
):
    outer = pools // INNER
    me = lax.axis_index("pool")
    con = lax.axis_index("con")
    my_in = lax.rem(me, INNER)
    my_out = me // INNER
    rows = pf_ref.shape[0]
    width = kmat.shape[2]
    feat = pf_ref.shape[1]
    row_tiles = mask_ref.shape[1]
    side = rows // row_tiles

    inner_ids = [(my_out * INNER + lax.rem(my_in + k, INNER), con) for k in range(INNER)]
    outer_ids = [(lax.rem(my_out + k, outer) * INNER + my_in, con) for k in range(outer)]
    con_ids = [(me, lax.rem(con + k, cons)) for k in range(cons)]

    barrier = pltpu.get_barrier_semaphore()
    peers = inner_ids[1:] + outer_ids[1:] + con_ids[1:]
    for peer in peers:
        pl.semaphore_signal(barrier, inc=1, device_id=peer, device_id_type=MESH)

    pending = []

    def send(src, dst, sems, at, peer):
        copy = pltpu.make_async_remote_copy(
            src_ref=src, dst_ref=dst, send_sem=sems.at[(0,) + at], recv_sem=sems.at[(1,) + at],
            device_id=peer, device_id_type=MESH,
        )
        copy.start()
        pending.append(copy)
        return copy

    def kernel_block(dst, feat_rows, feat_cols, mask_of):
        for tile in range(row_tiles):
            at = slice(tile * side, (tile + 1) * side)
            scores = dot(feat_rows(at), feat_cols, NT)
            dst[at, :] = (jnp.exp2(scores * (SCALE * math.log2(math.e))) * mask_of(tile)).astype(BF16)

    def own_block(j, carry):
        kernel_block(
            kmat.at[j], lambda at: pf_ref[at, :], cf_ref[j], lambda tile: mask_ref[j, tile : tile + 1, :]
        )
        return carry

    lax.fori_loop(0, INNER, own_block, 0)
    pft[...] = pf_ref[...].astype(F32).T

    def column_sums(weights, step):
        lhs = split_rows(weights)

        def body(j, carry):
            out = dot(lhs, kmat[j], NN)
            col_part[step, j] = out[0:1] + out[1:2]
            return carry

        lax.fori_loop(0, INNER, body, 0)

    def row_sums(vec):
        def body(j, total):
            return total + dot(split_rows(vec[j]), kmat[j], NT)

        total = lax.fori_loop(0, INNER, body, jnp.zeros((8, rows), F32))
        return total[0:1] + total[1:2]

    def reduce_columns(step, after_inner=None, between=None):
        copies = [
            send(col_part.at[step], col_in.at[step, k - 1], col_sem, (step, k - 1), inner_ids[k])
            for k in range(1, INNER)
        ]
        if between is not None:
            between()
        for copy in copies:
            copy.wait_recv()
        total = col_part[step]
        for k in range(INNER - 1):
            total = total + col_in[step, k]
        mid_part[step] = total
        copies = [
            send(mid_part.at[step], mid_in.at[step, k - 1], mid_sem, (step, k - 1), outer_ids[k])
            for k in range(1, outer)
        ]
        if after_inner is not None:
            after_inner()
        for copy in copies:
            copy.wait_recv()
        for k in range(outer - 1):
            total = total + mid_in[step, k]
        return total

    def reduce_rows(step, part):
        row_part[step] = part
        copies = [
            send(row_part.at[step], row_in.at[step, k - 1], row_sem, (step, k - 1), con_ids[k])
            for k in range(1, cons)
        ]
        for copy in copies:
            copy.wait_recv()
        for k in range(cons - 1):
            part = part + row_in[step, k]
        return part

    vec_copies = []

    def share_rows(which, value):
        row_vec[which] = value
        for k in range(1, INNER):
            vec_copies.append(
                send(row_vec.at[which], row_vec_in.at[k - 1, which], vec_sem, (which, k - 1), inner_ids[k])
            )

    feat_copies = []

    def share_features():
        for k in range(1, INNER):
            feat_copies.append(send(pft, pft_in.at[k - 1], feat_sem, (k - 1,), inner_ids[k]))
            feat_copies.append(
                send(
                    mask_ref.at[lax.rem(my_in + k, INNER)], mask_in.at[k - 1], mask_sem, (k - 1,), inner_ids[k]
                )
            )

    def peer_blocks():
        for copy in feat_copies:
            copy.wait_recv()
        for k in range(INNER - 1):
            rows_k = pft_in[k].T.astype(BF16)
            kernel_block(
                kpeer.at[k], lambda at: rows_k[at, :], cf_ref[my_in],
                lambda tile: mask_in[k, tile : tile + 1, :],
            )

    demand = caps_ref[...].astype(F32)
    supply = supply_ref[...]
    ones = jnp.ones((1, rows), F32)

    column_sums(ones, 0)
    pl.semaphore_wait(barrier, len(peers))
    vee[0] = demand / reduce_columns(0, after_inner=share_features)
    r1 = reduce_rows(0, row_sums(vee.at[0]))
    u1 = supply / r1
    share_rows(0, u1)
    column_sums(u1, 1)
    vee[1] = demand / reduce_columns(1, between=peer_blocks)
    r2 = reduce_rows(1, row_sums(vee.at[1]))
    rbar2 = -glp_ref[...] / r2
    share_rows(1, rbar2)
    column_sums(rbar2, 2)
    s2 = reduce_columns(2)
    v2 = vee[1]
    cbar[1] = -(glc_ref[...] / v2 + s2) * v2 * v2 / demand
    ubar = reduce_rows(2, row_sums(cbar.at[1]))
    rbar1 = -ubar * u1 / r1
    share_rows(2, rbar1)
    column_sums(rbar1, 3)

    def build_left():
        for copy in vec_copies:
            copy.wait_recv()
        fill_rows(left.at[0], left_rows([rbar2, u1, rbar1, ones]))
        for k in range(1, INNER):
            fill_rows(
                left.at[k],
                left_rows([row_vec_in[k - 1, 1], row_vec_in[k - 1, 0], row_vec_in[k - 1, 2], ones]),
            )

    s1 = reduce_columns(3, after_inner=build_left)
    v1 = vee[0]
    cbar[0] = -s1 * v1 * v1 / demand

    for j in range(INNER):
        fill_rows(right.at[j], right_rows([vee[1, j], cbar[1, j], vee[0, j], cbar[0, j]]))

    rhs = right[my_in].astype(BF16)
    weights = dot(left[0].astype(BF16), rhs, TN)
    grad = (kmat[my_in].astype(F32) * weights).astype(BF16)
    total = dot(pft[...].astype(BF16), grad, NN)

    def peer_grad(k, total):
        weights = dot(left[k + 1].astype(BF16), rhs, TN)
        grad = (kpeer[k].astype(F32) * weights).astype(BF16)
        return total + dot(pft_in[k].astype(BF16), grad, NN)

    total = lax.fori_loop(0, INNER - 1, peer_grad, total) * SCALE
    share = feat // outer
    for o in range(outer):
        rs_part[o] = total[o * share : (o + 1) * share]
    rs_copies = [
        send(rs_part.at[lax.rem(my_out + k, outer)], rs_in.at[k - 1], rs_sem, (k - 1,), outer_ids[k])
        for k in range(1, outer)
    ]

    lhs = left[0].astype(BF16)

    def pool_grad_part(j, total):
        weights = dot(lhs, right[j].astype(BF16), TN)
        grad = (kmat[j].astype(F32) * weights).astype(BF16)
        return total + dot(grad, cf_ref[j], NN)

    pg = lax.fori_loop(0, INNER, pool_grad_part, jnp.zeros((rows, feat), F32)) * SCALE
    pg_part[...] = pg
    pg_copies = [
        send(pg_part, pg_in.at[k - 1], pg_sem, (k - 1,), con_ids[k]) for k in range(1, cons)
    ]

    for copy in rs_copies:
        copy.wait_recv()
    mine = rs_part[my_out]
    for k in range(outer - 1):
        mine = mine + rs_in[k]
    gathered[my_in, my_out] = mine
    z_copies = []
    plane_copies = [[] for _ in range(INNER)]

    def spread(slot, k):
        for other in range(1, INNER):
            plane_copies[other].append(send(slot, slot, agp_sem, (k, other - 1), inner_ids[other]))

    slot = gathered.at[my_in, my_out]
    for k in range(1, outer):
        z_copies.append(send(slot, slot, agz_sem, (k - 1,), outer_ids[k]))
    spread(slot, 0)
    for k in range(1, outer):
        z_copies[k - 1].wait_recv()
        spread(gathered.at[my_in, lax.rem(my_out + outer - k, outer)], k)

    for copy in pg_copies:
        copy.wait_recv()
    pg = pg_part[...]
    for k in range(cons - 1):
        pg = pg + pg_in[k]
    pool_out[...] = pg

    def put_out(index):
        block = jnp.concatenate([gathered[index, o] for o in range(outer)], axis=0)
        contract_out[pl.ds(pl.multiple_of(index * width, width), width), :] = block.T

    put_out(my_in)
    for other in range(1, INNER):
        for copy in plane_copies[other]:
            copy.wait_recv()
        put_out(lax.rem(my_in + INNER - other, INNER))
    for copy in pending:
        copy.wait_send()


def shards(pools, cons, pool_feat, contract_feat, supply, caps, eligible, grad_log_pool, grad_log_contract):
    rows, feat = pool_feat.shape
    cols = contract_feat.shape[0]
    outer = pools // INNER
    width = cols // INNER
    row_tiles, col_tiles = eligible.shape
    mask = eligible.astype(F32)
    mask = jnp.repeat(mask, cols // col_tiles, axis=1).reshape(row_tiles, INNER, width).transpose(1, 0, 2)
    share = feat // outer
    vmem = pl.BlockSpec(memory_space=pltpu.VMEM)
    dma = pltpu.SemaphoreType.DMA
    return pl.pallas_call(
        functools.partial(kernel, pools, cons),
        out_shape=(
            jax.ShapeDtypeStruct((rows, feat), F32),
            jax.ShapeDtypeStruct((cols, feat), F32),
        ),
        in_specs=[vmem] * 7,
        out_specs=(vmem, vmem),
        scratch_shapes=[
            pltpu.VMEM((INNER, rows, width), BF16),
            pltpu.VMEM((INNER - 1, rows, width), BF16),
            pltpu.VMEM((feat, rows), F32),
            pltpu.VMEM((INNER - 1, feat, rows), F32),
            pltpu.VMEM((INNER - 1, row_tiles, width), F32),
            pltpu.VMEM((4, INNER, 1, width), F32),
            pltpu.VMEM((4, INNER - 1, INNER, 1, width), F32),
            pltpu.VMEM((4, INNER, 1, width), F32),
            pltpu.VMEM((4, outer - 1, INNER, 1, width), F32),
            pltpu.VMEM((3, 1, rows), F32),
            pltpu.VMEM((3, cons - 1, 1, rows), F32),
            pltpu.VMEM((3, 1, rows), F32),
            pltpu.VMEM((INNER - 1, 3, 1, rows), F32),
            pltpu.VMEM((2, INNER, 1, width), F32),
            pltpu.VMEM((2, INNER, 1, width), F32),
            pltpu.VMEM((INNER, 16, rows), F32),
            pltpu.VMEM((INNER, 16, width), F32),
            pltpu.VMEM((rows, feat), F32),
            pltpu.VMEM((cons - 1, rows, feat), F32),
            pltpu.VMEM((outer, share, width), F32),
            pltpu.VMEM((outer - 1, share, width), F32),
            pltpu.VMEM((INNER, outer, share, width), F32),
            dma((2, 4, INNER - 1)),
            dma((2, 4, outer - 1)),
            dma((2, 3, cons - 1)),
            dma((2, 3, INNER - 1)),
            dma((2, INNER - 1)),
            dma((2, INNER - 1)),
            dma((2, cons - 1)),
            dma((2, outer - 1)),
            dma((2, outer - 1)),
            dma((2, outer, INNER - 1)),
        ],
        compiler_params=pltpu.CompilerParams(
            collective_id=0, has_side_effects=True, vmem_limit_bytes=56 * 1024 * 1024
        ),
        name="sinkhorn",
    )(
        pool_feat,
        contract_feat.reshape(INNER, width, feat),
        supply.reshape(1, rows),
        caps.reshape(INNER, 1, width),
        mask,
        grad_log_pool.reshape(1, rows),
        grad_log_contract.reshape(INNER, 1, width),
    )


def solution(mesh):
    placed = (
        P("pool", None),
        P("con", None),
        P("pool"),
        P("con"),
        P("pool", "con"),
        P("pool"),
        P("con"),
    )
    return jax.shard_map(
        functools.partial(shards, mesh.shape["pool"], mesh.shape["con"]),
        mesh=mesh,
        in_specs=placed,
        out_specs=(P("pool", None), P("con", None)),
        check_vma=False,
    )
```

time: 606 us -> 80.2 us (0.13)
  blocking collectives: 301 us -> 0 us
  waiting for transfers between devices: 127 us -> 0 us
  matrix products: 109 us -> 0 us
  Pallas kernels: 0 us -> 68.9 us
  local copies, waits for them, and re-layouts: 49 us -> 9.59 us
  between operations: 15.7 us -> 0.65 us
    psum x7 -> x0, blocking collectives: 301 us -> none  [the longest x4 294 us: column_step(): summed = lax.psum(partial_sum, 'pool')]
    dot_general x72 -> x0, matrix products: 109 us -> none  [the longest x32 43.5 us: kernel_tile(): jnp.dot(pool_feat, feat_block.T, preferred_element_type=jnp.float32) * 0.125]
    reduce_scatter x1 -> x0, waiting for transfers between devices: 74.6 us -> none  [shards(): lax.psum_scatter(contract_part, 'pool', scatter_dimension=0, tiled=True)]
    pallas_call x0 -> x1, Pallas kernels: none -> 68.9 us  [shards(): pl.pallas_call(functools.partial(kernel, pools, cons), out_shape=(jax.Sha...]
    all_gather x1 -> x0, waiting for transfers between devices: 51.8 us -> none  [shards(): contract_grad = lax.all_gather(shared, 'pool', axis=0, tiled=True)]
    dynamic_update_slice x24 -> x0, local copies, waits for them, and re-layouts: 25.6 us -> none  [the longest x8 24.5 us: shards(): lax.scan(final_block, jnp.zeros((row_count, width_feat), jnp.float32), (f...]
    mul x32 -> x0, local copies, waits for them, and re-layouts: 10.8 us -> none  [kernel_tile(): values.reshape(row_count // tile_side, tile_side, col_count // tile_side,...]
  transfers between devices with their start and end apart: 3 -> 0, of which waited for: 2 -> 0; matrix products, arithmetic and copies ran while one was open for 0% -> 0% of each run, Pallas kernels for 0% -> 0%
where the time goes in v1:
time: 80.2 us; the launch traced here: 79.8 us
  Pallas kernels  68.9 us (86%)
  local copies, waits for them, and re-layouts  9.59 us (12%)
    pallas_call x1, Pallas kernels, shards(): pl.pallas_call(functools.partial(kernel, pools, cons), out_shape=(jax.Sha...  68.9 us
    pallas_call x2, local copies, waits for them, and re-layouts, shards(): pl.pallas_call(functools.partial(kernel, pools, cons), out_shape=(jax.Sha...  4.87 us
    unnamed x2, local copies, waits for them, and re-layouts  3.95 us

profile of v1, /device:TPU:0, one launch (start us, length us, event | category | flops | bytes accessed | tf_op | source)
XLA Modules:
  0.0 79.8 jit_solution(3596160657864135678)
XLA Ops:
  0.6 0.7 convert_element_type.3
  1.3 0.1 broadcast_in_dim.3
  1.4 0.7 copy.19
  2.1 1.6 %copy.15.pf_ref = bf16[512,64]{1,0:T(8,128)(2,1)} copy(bf16[512,64]{0,1:T(8,128)(2,1)} %param.7) | data formatting | bytes 131072 | tf_op args[0]
  3.7 2.4 %copy.13 = bf16[4096,64]{1,0:T(8,128)(2,1)} copy(bf16[4096,64]{0,1:T(8,128)(2,1)} %param.8) | data formatting | bytes 1048576 | tf_op args[1]
  6.0 68.9 %sinkhorn.1 = (f32[512,64]{1,0:T(8,128)}, f32[4096,64]{1,0:T(8,128)}) custom-call(bf16[512,64]{1,0:T(8,128)(2,1)} %copy.15.pf_ref, bf16[4,1024,64]{2,1,0:T(8,128)(2,1)} %bitcast.8, f32[1,512]{1,0:T(1,128)} %bitcast.12, s32[4,1,1024]{2,1,0:T(1,128)} %bitcast.10, f32[4,4,1024]{2,1,0:T(4,128)} %bitcast.9, f32[1,512]{1,0:T(1,128)} %bitcast.13, ...), custom_call_target="tpu_custom_call" | custom-call | tf_op jit(solution)/shard_map/sinkhorn/pallas_call | solution.py:322
  75.0 1.7 %copy.16 = f32[512,64]{0,1:T(8,128)} copy(f32[512,64]{1,0:T(8,128)} %get-tuple-element.4) | data formatting | bytes 262144 | tf_op jit(solution)/shard_map/sinkhorn/pallas_call | solution.py:322
  76.7 3.1 %copy.17 = f32[4096,64]{0,1:T(8,128)} copy(f32[4096,64]{1,0:T(8,128)} %get-tuple-element.5) | data formatting | bytes 2097152 | tf_op jit(solution)/shard_map/sinkhorn/pallas_call | solution.py:322
  (1 shorter events, 0.0 us)
